TPU v7x, 128 devices: a whole 4x4x4 slice. The times are simulated.
128 devices in a mesh: tm: 16 (over z, y), col: 8 (over x, core).
Axes of the slice: x: 4, y: 4, z: 4, core: 2. Of those that a mesh axis runs over, the one named last changes fastest.
Arguments:
- block_values: bfloat16 [8, 32768, 128], P('col', 'tm'), may hold values from -6 to 6
- block_shifts: bfloat16 [8, 32768, 128], P('col', 'tm'), may hold values from -1 to 1
- block_sensor: int32 [8, 32768], P('col', 'tm'), may hold values from 0 to 2047
- block_window: int32 [8, 32768], P('col', 'tm'), may hold values from 0 to 3
- block_owner: int32 [8, 32768, 1], P('col', 'tm'), may hold values from 0 to 15; in each aligned block of 2048 rows (0 to 2047, 2048 to 4095, ..., all dimensions but the last counted through in order) at most 192 rows name the same one
- block_counts: int32 [8, 16], P('col', 'tm'), may hold values from 1536 to 2048
- calibration: bfloat16 [16384, 4096], P('tm', 'col'), may hold values from -0.046875 to 0.046875
Outputs:
- calibrated: bfloat16 [8192, 4096], P('tm', 'col')
Inputs may be any that keep to these rules, and one draw needn't show every extreme that they name: `block_owner`: among the 2048 block slots of one device, at most 192 name the same owner, a bound that some block reaches. The live blocks of device (tm t, col c) are its first block_counts[c, t] slots.
All inputs are finite; a program needn't handle non-finite values.
Results may differ from a plain program's by a relative error of at most 0.015.
Values may be sent and summed in bfloat16 or wider, within the bound.
A program may use at most 128 MiB of HBM per device.

v0:
```python
import jax
import jax.numpy as jnp
from jax import lax
from jax.sharding import Mesh
from jax.sharding import PartitionSpec as P

SENSORS = 16384
ROWS_DEV = 512
TM = ("tm_0", "tm_1")


def cut_rows(length, count):
    unit = 8 if length >= 8 * count else 1
    return [length // unit * k // count * unit for k in range(1, count)]


def gather_in_order(shard, axes, sequence):
    parts = shard[None]
    for k in sequence:
        parts = lax.all_gather(parts, axes[k], axis=0, tiled=True)
    carried = [lax.axis_size(axes[k]) for k in reversed(sequence)]
    parts = parts.reshape(*carried, *shard.shape)
    turned = sorted(range(len(sequence)), key=lambda place: sequence[len(sequence) - 1 - place])
    return parts.transpose(*turned, *range(len(sequence), parts.ndim)).reshape(-1, *shard.shape)


def joined_along(parts, dim):
    lengths = list(parts.shape[1:])
    lengths[dim] *= parts.shape[0]
    return jnp.moveaxis(parts, 0, dim).reshape(lengths)


def gather_all_axes(shard, axes, dim):
    numbers = list(range(len(axes)))[::-1]
    cut = shard.shape.index(max(shard.shape[:-1] or shard.shape))
    edges = [0, *cut_rows(shard.shape[cut], len(axes)), shard.shape[cut]]
    outs = []
    for k, (start, end) in enumerate(zip(edges, edges[1:])):
        if end > start:
            slab = lax.slice_in_dim(shard, start, end, axis=cut)
            outs.append(gather_in_order(slab, axes, numbers[k:] + numbers[:k]))
    return joined_along(jnp.concatenate(outs, axis=cut + 1), dim)


def spread_samples(values, shifts):
    samples = values.astype(jnp.float32)
    offsets = shifts.astype(jnp.float32)
    result = jnp.zeros(samples.shape, jnp.float32)
    lead = [(0, 0)] * (samples.ndim - 1)
    for displace in (-1, 0, 1):
        weight = jnp.maximum(0.0, 1.0 - jnp.abs(offsets - displace)).astype(jnp.bfloat16)
        weight = lax.optimization_barrier(weight).astype(jnp.float32)
        product = weight * samples
        if displace == 1:
            result = result + jnp.pad(product[..., :-1], lead + [(1, 0)])
        elif displace == -1:
            result = jnp.pad(product[..., 1:], lead + [(0, 1)])
        else:
            result = result + product
    return result


def spread_slots(moved_slots):
    return spread_samples(moved_slots[:, :, 0], moved_slots[:, :, 1])


def per_device(
    block_values, block_shifts, block_sensor, block_window, block_owner, block_counts, calibration
):
    values = block_values[0]
    shifts = block_shifts[0]
    blocks = values.shape[0]
    length = values.shape[1]
    owners = lax.axis_size(TM)
    group_size = SENSORS // lax.axis_size("col")
    windows = ROWS_DEV // length
    capacity = blocks * 3 // (2 * owners)
    slot_total = owners * capacity
    block_index = lax.iota(jnp.int32, blocks)
    is_live = block_index < block_counts[0, 0]
    values = jnp.where(is_live[:, None], values, jnp.zeros_like(values))
    owner_ids = block_owner[0, :, 0]
    owner_onehot = (owner_ids[:, None] == lax.iota(jnp.int32, owners)[None, :]).astype(jnp.bfloat16)
    lower_mask = (block_index[:, None] > block_index[None, :]).astype(jnp.bfloat16)
    earlier = jnp.dot(lower_mask, owner_onehot, preferred_element_type=jnp.float32)
    slot_rank = jnp.sum(earlier * owner_onehot.astype(jnp.float32), axis=1).astype(jnp.int32)
    slot_index = owner_ids * capacity + slot_rank
    slot_match = slot_index[None, :] == lax.iota(jnp.int32, slot_total)[:, None]
    source = jnp.max(jnp.where(slot_match, block_index[None, :], -1), axis=1)
    filled = source >= 0
    source_row = jnp.maximum(source, 0)
    row_keys = block_window[0] * group_size + block_sensor[0]
    payload = jnp.stack((values, shifts), axis=1)
    outgoing = jnp.where(
        filled[:, None, None], jnp.take(payload, source_row, axis=0), jnp.zeros((), jnp.bfloat16)
    )
    outgoing = outgoing.reshape(owners, capacity, 2, length)
    outgoing_keys = jnp.where(filled, jnp.take(row_keys, source_row, axis=0), 0).reshape(
        owners, capacity
    )
    contribution = spread_slots(
        lax.all_to_all(outgoing, TM, split_axis=0, concat_axis=0, tiled=True)
    )
    incoming_keys = lax.all_to_all(outgoing_keys, TM, split_axis=0, concat_axis=0, tiled=True)
    flat_keys = incoming_keys.reshape(-1)
    flat_contrib = contribution.reshape(-1, length)
    upper_part = flat_contrib.astype(jnp.bfloat16)
    lower_part = (flat_contrib - upper_part.astype(jnp.float32)).astype(jnp.bfloat16)
    sensor_iota = lax.iota(jnp.int32, group_size)
    window_rows = []
    for window in range(windows):
        target = flat_keys - window * group_size
        place_onehot = (target[:, None] == sensor_iota[None, :]).astype(jnp.bfloat16)
        dims = (((0,), (0,)), ((), ()))
        window_sum = lax.dot_general(
            upper_part, place_onehot, dims, preferred_element_type=jnp.float32
        )
        window_sum = window_sum + lax.dot_general(
            lower_part, place_onehot, dims, preferred_element_type=jnp.float32
        )
        window_rows.append(window_sum)
    aligned = jnp.concatenate(window_rows, axis=0).astype(jnp.bfloat16)
    cal_rows = gather_all_axes(calibration, TM, 0)
    running = jnp.dot(
        lax.all_gather(aligned, "col", axis=1, tiled=True),
        cal_rows,
        preferred_element_type=jnp.float32,
    )
    return running.astype(jnp.bfloat16)


def solution(mesh):
    torus = Mesh(mesh.devices.reshape(4, 4, mesh.shape["col"]), ("tm_0", "tm_1", "col"))
    in_specs = (
        P("col", TM, None),
        P("col", TM, None),
        P("col", TM),
        P("col", TM),
        P("col", TM, None),
        P("col", TM),
        P(TM, "col"),
    )
    out_specs = P(TM, "col")
    return jax.shard_map(
        per_device, mesh=torus, in_specs=in_specs, out_specs=out_specs, check_vma=False
    )
```

profile of v0, /device:TPU:1, one launch (start us, length us, event | category | flops | bytes accessed | tf_op | source)
XLA Modules:
  0.0 359.0 jit_solution(3384023761466500668)
XLA Ops:
  6.5 0.0 copy-start.2
  6.5 0.0 all-gather.16.cloned.1.call-start
  6.5 2.3 fusion.45
  8.8 0.0 all-gather.16.cloned.1.call-update
  8.8 0.0 all-gather.14.cloned.1.call-start
  8.9 0.7 all-gather.14.cloned.1.call-update
  9.6 0.0 all-gather.12.cloned.1.call-start
  9.6 33.4 %all-gather.16.cloned.1.call-done = bf16[2048,512]{1,0:T(8,128)(2,1)} async-done(((bf16[512,512]{1,0:T(8,128)(2,1)}), bf16[2048,512]{1,0:T(8,128)(2,1)}) %all-gather.16.cloned.1.call-update) | async-done | bytes 2097168 | tf_op jit(solution)/shard_map/all_gather | solution.py:20
  43.1 0.0 all-gather.12.cloned.1.call-update
  43.1 0.0 copy-start.3
  43.1 0.0 copy-start.4
  43.1 0.0 all-gather.10.cloned.1.call-start
  43.2 32.3 %all-gather.14.cloned.1.call-done = bf16[2048,512]{1,0:T(8,128)(2,1)} async-done(((bf16[512,512]{1,0:T(8,128)(2,1)}), bf16[2048,512]{1,0:T(8,128)(2,1)}) %all-gather.14.cloned.1.call-update) | async-done | bytes 2097168 | tf_op jit(solution)/shard_map/all_gather | solution.py:20
  75.4 0.0 all-gather.10.cloned.1.call-update
  75.4 0.0 copy-done.2
  75.4 1.5 fusion.38
  77.0 3.4 select_reduce_fusion
  80.4 0.0 copy-done.3
  80.4 0.0 copy-done.4
  80.4 0.0 copy-start
  80.4 0.0 copy-start.1
  80.4 17.4 %gather_fusion.1 = s32[3072]{0:T(1024)S(1)} fusion(s32[2048]{0:T(1024)S(1)} %bitcast.37, s32[3072]{0:T(1024)S(1)} %maximum_clamp_fusion), kind=kCustom, calls=%fused_computation.1 | custom fusion | bytes 36864 | tf_op jit(solution)/shard_map/jit(_take)/gather | solution.py:98
  97.9 0.7 select_n.64
  98.5 5.7 %all-to-all-start.1 = ((s32[16,1,192]{2,1,0:T(1,128)}), s32[16,1,192]{2,1,0:T(1,128)S(1)}, u32[]{:S(2)}, u32[]{:S(2)}) async-start(s32[16,1,192]{2,1,0:T(1,128)} %select_n.64), calls=%async_computation.1 | async-start | bytes 32768 | tf_op jit(solution)/shard_map/all_to_all | solution.py:104
  104.9 0.1 le.30
  104.9 0.1 ge.33
  105.0 0.0 copy-done
  105.0 8.1 %copy.20 = bf16[2048,1,128]{2,1,0:T(2,128)(2,1)S(1)} copy(bf16[2048,1,128]{2,0,1:T(8,128)(2,1)S(1)} %bitcast.46) | data formatting | bytes 1048576 | tf_op jit(solution)/shard_map/stack;squeeze | solution.py:93
  113.2 0.0 copy-done.1
  113.2 15.2 %broadcast_select_fusion.2 = bf16[2048,1,128]{2,1,0:T(2,128)(2,1)S(1)} fusion(pred[2048]{0:T(1024)(128)(4,1)S(1)} %iota_compare_fusion.37, bf16[2048,1,128]{2,0,1:T(8,128)(2,1)S(1)} %bitcast.47), kind=kLoop, calls=%fused_computation.42 | loop fusion | flops 262144 | bytes 1050624 | tf_op jit(solution)/shard_map/jit(_where)/select_n | solution.py:81
  128.4 2.4 pad_maximum_fusion.2
  130.8 10.4 %gather_fusion = bf16[3072,2,128]{2,1,0:T(2,128)(2,1)S(1)} fusion(bf16[2048,2,128]{2,1,0:T(2,128)(2,1)S(1)} %pad_maximum_fusion.2, s32[3072]{0:T(1024)S(1)} %maximum_clamp_fusion), kind=kCustom, calls=%fused_computation | custom fusion | bytes 3158016 | tf_op jit(solution)/shard_map/jit(_take)/gather | solution.py:95
  141.3 9.9 %broadcast_select_fusion.1 = bf16[16,192,2,128]{3,2,1,0:T(2,128)(2,1)} fusion(pred[16,192]{1,0:T(8,128)(4,1)S(1)} %ge.33, bf16[16,192,2,128]{3,2,1,0:T(2,128)(2,1)S(1)} %bitcast.43, pred[16,192]{1,0:T(8,128)(4,1)S(1)} %le.30), kind=kLoop, calls=%fused_computation.28 | loop fusion | flops 1572864 | bytes 3151872 | tf_op jit(solution)/shard_map/jit(_where)/select_n | solution.py:94
  151.2 0.0 all-to-all-done.1
  151.2 6.7 %all-to-all-start = ((bf16[16,192,2,128]{3,2,1,0:T(2,128)(2,1)}), bf16[16,192,2,128]{3,2,1,0:T(2,128)(2,1)S(1)}, u32[]{:S(2)}, u32[]{:S(2)}) async-start(bf16[16,192,2,128]{3,2,1,0:T(2,128)(2,1)} %broadcast_select_fusion.1), calls=%async_computation | async-start | bytes 3145728 | tf_op jit(solution)/shard_map/all_to_all | solution.py:102
  158.0 0.0 all-gather.8.cloned.1.call-start
  158.1 0.1 eq.36
  158.2 20.8 %all-to-all-done = bf16[16,192,2,128]{3,2,1,0:T(2,128)(2,1)S(1)} async-done(((bf16[16,192,2,128]{3,2,1,0:T(2,128)(2,1)}), bf16[16,192,2,128]{3,2,1,0:T(2,128)(2,1)S(1)}, u32[]{:S(2)}, u32[]{:S(2)}) %all-to-all-start) | async-done | bytes 1572896 | tf_op jit(solution)/shard_map/all_to_all | solution.py:102
  178.9 2.6 fusion.44
  181.5 0.8 fusion.41
  182.4 0.8 slice_multiply_fusion.1
  183.2 0.6 pad_add_fusion
  183.8 0.2 fusion.37
  184.0 5.3 %fusion.6 = f32[128,2048]{1,0:T(8,128)S(1)} fusion(bf16[3072,128]{1,0:T(8,128)(2,1)S(1)} %get-tuple-element.8, s32[3072]{0:T(1024)S(1)} %eq.36), kind=kOutput, calls=%fused_computation.12 | convolution fusion | flops 1616904192 | bytes 1847296 | tf_op jit(solution)/shard_map/dot_general | solution.py:118
  189.3 5.3 %fusion = f32[128,2048]{1,0:T(8,128)S(1)} fusion(bf16[3072,128]{1,0:T(8,128)(2,1)S(1)} %get-tuple-element.8, s32[3072]{0:T(1024)S(1)} %get-tuple-element.20), kind=kOutput, calls=%fused_computation.3 | convolution fusion | flops 1616904192 | bytes 1847296 | tf_op jit(solution)/shard_map/dot_general | solution.py:118
  194.7 5.5 %fusion.2 = f32[128,2048]{1,0:T(8,128)S(1)} fusion(bf16[3072,128]{1,0:T(8,128)(2,1)S(1)} %get-tuple-element.8, s32[3072]{0:T(1024)S(1)} %get-tuple-element.21), kind=kOutput, calls=%fused_computation.6 | convolution fusion | flops 1616904192 | bytes 1847296 | tf_op jit(solution)/shard_map/dot_general | solution.py:118
  200.2 5.3 %fusion.4 = f32[128,2048]{1,0:T(8,128)S(1)} fusion(bf16[3072,128]{1,0:T(8,128)(2,1)S(1)} %get-tuple-element.8, s32[3072]{0:T(1024)S(1)} %get-tuple-element.19), kind=kOutput, calls=%fused_computation.9 | convolution fusion | flops 1616904192 | bytes 1847296 | tf_op jit(solution)/shard_map/dot_general | solution.py:118
  205.5 5.5 %fusion.21 = bf16[128,2048]{1,0:T(8,128)(2,1)S(1)} fusion(f32[128,2048]{1,0:T(8,128)S(1)} %fusion, bf16[3072,128]{1,0:T(8,128)(2,1)S(1)} %get-tuple-element.9, s32[3072]{0:T(1024)S(1)} %get-tuple-element.20), kind=kOutput, calls=%fused_computation.33 | convolution fusion | flops 1617428480 | bytes 2371584 | tf_op jit(solution)/shard_map/dot_general | solution.py:115
  211.1 5.3 %fusion.22 = bf16[128,2048]{1,0:T(8,128)(2,1)S(1)} fusion(f32[128,2048]{1,0:T(8,128)S(1)} %fusion.2, bf16[3072,128]{1,0:T(8,128)(2,1)S(1)} %get-tuple-element.9, s32[3072]{0:T(1024)S(1)} %get-tuple-element.21), kind=kOutput, calls=%fused_computation.34 | convolution fusion | flops 1617428480 | bytes 2371584 | tf_op jit(solution)/shard_map/dot_general | solution.py:115
  216.4 5.3 %fusion.23 = bf16[128,2048]{1,0:T(8,128)(2,1)S(1)} fusion(f32[128,2048]{1,0:T(8,128)S(1)} %fusion.4, bf16[3072,128]{1,0:T(8,128)(2,1)S(1)} %get-tuple-element.9, s32[3072]{0:T(1024)S(1)} %get-tuple-element.19), kind=kOutput, calls=%fused_computation.35 | convolution fusion | flops 1617428480 | bytes 2371584 | tf_op jit(solution)/shard_map/dot_general | solution.py:115
  221.8 5.6 %fusion.24 = bf16[128,2048]{1,0:T(8,128)(2,1)S(1)} fusion(f32[128,2048]{1,0:T(8,128)S(1)} %fusion.6, bf16[3072,128]{1,0:T(8,128)(2,1)S(1)} %get-tuple-element.9, s32[3072]{0:T(1024)S(1)} %eq.36), kind=kOutput, calls=%fused_computation.36 | convolution fusion | flops 1617428480 | bytes 2371584 | tf_op jit(solution)/shard_map/dot_general | solution.py:115
  227.4 1.4 pad_maximum_fusion.1
  228.8 0.0 all-gather.8.cloned.1.call-update
  228.8 0.0 all-gather.12.cloned.1.call-done
  228.9 7.3 %copy.22 = bf16[4,4,512,512]{3,2,0,1:T(8,128)(2,1)} copy(bf16[4,4,512,512]{3,2,1,0:T(8,128)(2,1)} %bitcast.42) | data formatting | bytes 16777216 | tf_op jit(solution)/shard_map/reshape | solution.py:22
  236.2 11.4 %all-gather.10.cloned.1.call-done = bf16[16,512,512]{2,1,0:T(8,128)(2,1)} async-done(((bf16[4,512,512]{2,1,0:T(8,128)(2,1)}), bf16[16,512,512]{2,1,0:T(8,128)(2,1)}) %all-gather.10.cloned.1.call-update) | async-done | bytes 8388624 | tf_op jit(solution)/shard_map/all_gather | solution.py:20
  247.6 13.9 %pad_maximum_fusion = bf16[16,1024,512]{2,1,0:T(8,128)(2,1)} fusion(bf16[16,512,512]{2,1,0:T(8,128)(2,1)} %bitcast.38, bf16[16,512,512]{2,1,0:T(8,128)(2,1)} %all-gather.10.cloned.1.call-done), kind=kLoop, calls=%fused_computation.16 | loop fusion | flops 33554432 | bytes 33554432 | tf_op jit(solution)/shard_map/concatenate | solution.py:42
  261.5 72.7 %all-gather.8.cloned.1.call-done = bf16[512,16384]{1,0:T(8,128)(2,1)} async-done(((bf16[512,2048]{1,0:T(8,128)(2,1)}), bf16[512,16384]{1,0:T(8,128)(2,1)}) %all-gather.8.cloned.1.call-update) | async-done | bytes 16777232 | tf_op jit(solution)/shard_map/all_gather | solution.py:125
  334.1 17.9 %convolution_convert_fusion = bf16[512,512]{1,0:T(8,128)(2,1)} fusion(bf16[512,16384]{1,0:T(8,128)(2,1)} %all-gather.8.cloned.1.call-done, bf16[16384,512]{1,0:T(8,128)(2,1)} %bitcast.41), kind=kOutput, calls=%fused_computation.61 | convolution fusion | flops 8590196736 | bytes 34078720 | tf_op jit(solution)/shard_map/dot_general | solution.py:124
  (7 shorter events, 0.1 us)
Async XLA Ops:
  6.5 68.9 %copy-start.2 = (s32[1,2048,1]{1,2,0:T(1,128)S(1)}, s32[1,2048,1]{1,2,0:T(1,128)}, u32[]{:S(2)}) copy-start(s32[1,2048,1]{1,2,0:T(1,128)} %param.11) | copy-start | bytes 24580
  6.5 36.5 %all-gather.16.cloned.1.call-start = ((), (), s32[]{:S(2)}) async-start(), calls=%async_computation.6 | async-start | bytes 2621440 | tf_op jit(solution)/shard_map/all_gather | solution.py:20
  8.8 66.6 %all-gather.14.cloned.1.call-start = ((), (), s32[]{:S(2)}) async-start(), calls=%async_computation.5 | async-start | bytes 2621440 | tf_op jit(solution)/shard_map/all_gather | solution.py:20
  9.6 219.3 %all-gather.12.cloned.1.call-start = ((), (), s32[]{:S(2)}) async-start(), calls=%async_computation.4 | async-start | bytes 10485760 | tf_op jit(solution)/shard_map/all_gather | solution.py:20
  43.1 37.3 %copy-start.3 = (s32[1,2048]{1,0:T(1,128)S(1)}, s32[1,2048]{1,0:T(1,128)}, u32[]{:S(2)}) copy-start(s32[1,2048]{1,0:T(1,128)} %param.9) | copy-start | bytes 24580
  43.1 37.3 %copy-start.4 = (s32[1,2048]{1,0:T(1,128)S(1)}, s32[1,2048]{1,0:T(1,128)}, u32[]{:S(2)}) copy-start(s32[1,2048]{1,0:T(1,128)} %param.10) | copy-start | bytes 24580
  43.1 204.5 %all-gather.10.cloned.1.call-start = ((), (), s32[]{:S(2)}) async-start(), calls=%async_computation.3 | async-start | bytes 10485760 | tf_op jit(solution)/shard_map/all_gather | solution.py:20
  80.4 24.6 %copy-start = (bf16[1,2048,128]{2,1,0:T(8,128)(2,1)S(1)}, bf16[1,2048,128]{2,1,0:T(8,128)(2,1)}, u32[]{:S(2)}) copy-start(bf16[1,2048,128]{2,1,0:T(8,128)(2,1)} %param.8) | copy-start | bytes 1572868
  80.4 32.8 %copy-start.1 = (bf16[1,2048,128]{2,1,0:T(8,128)(2,1)S(1)}, bf16[1,2048,128]{2,1,0:T(8,128)(2,1)}, u32[]{:S(2)}) copy-start(bf16[1,2048,128]{2,1,0:T(8,128)(2,1)} %param.7) | copy-start | bytes 1572868
  98.5 52.7 %all-to-all-start.1 = ((s32[16,1,192]{2,1,0:T(1,128)}), s32[16,1,192]{2,1,0:T(1,128)S(1)}, u32[]{:S(2)}, u32[]{:S(2)}) async-start(s32[16,1,192]{2,1,0:T(1,128)} %select_n.64), calls=%async_computation.1 | async-start | bytes 32768 | tf_op jit(solution)/shard_map/all_to_all | solution.py:104
  151.2 27.7 %all-to-all-start = ((bf16[16,192,2,128]{3,2,1,0:T(2,128)(2,1)}), bf16[16,192,2,128]{3,2,1,0:T(2,128)(2,1)S(1)}, u32[]{:S(2)}, u32[]{:S(2)}) async-start(bf16[16,192,2,128]{3,2,1,0:T(2,128)(2,1)} %broadcast_select_fusion.1), calls=%async_computation | async-start | bytes 3145728 | tf_op jit(solution)/shard_map/all_to_all | solution.py:102
  158.0 176.2 %all-gather.8.cloned.1.call-start = ((), (), s32[]{:S(2)}) async-start(), calls=%async_computation.2 | async-start | bytes 18874368 | tf_op jit(solution)/shard_map/all_gather | solution.py:125
Sparse Core Ops, SparseCore 0:
  9.0 34.0 all-gather.15
  44.7 30.6 all-gather.13
  77.1 83.2 all-gather.11
  161.9 85.6 all-gather.9
  249.1 84.9 all-gather.7
where the time goes:
time: 364 us; the launch traced here: 359 us
  waiting for transfers between devices  171 us (47%)
  matrix products  62.6 us (17%)
  other arithmetic  51.4 us (14%)
  local copies, waits for them, and re-layouts  46.6 us (13%)
  between operations  14.5 us (4%)
  starting transfers between devices  12.6 us (3%)
    all_gather x4, waiting for transfers between devices, gather_in_order(): parts = lax.all_gather(parts, axes[k], axis=0, tiled=True)  77.1 us
    all_gather x1, waiting for transfers between devices, per_device(): lax.all_gather(aligned, 'col', axis=1, tiled=True)  72.7 us
    dot_general x4, matrix products, per_device(): lax.dot_general(upper_part, place_onehot, dims, preferred_element_type=jn...  21.8 us
    dot_general x4, matrix products, per_device(): lax.dot_general(lower_part, place_onehot, dims, preferred_element_type=jn...  21.5 us
    all_to_all x1, waiting for transfers between devices, per_device(): lax.all_to_all(outgoing, TM, split_axis=0, concat_axis=0, tiled=True)  20.8 us
    dot_general x1, matrix products, per_device(): jnp.dot(lax.all_gather(aligned, 'col', axis=1, tiled=True), cal_rows, pre...  17.9 us
    gather x1, local copies, waits for them, and re-layouts, per_device(): jnp.take(row_keys, source_row, axis=0)  17.4 us
    select_n x1, other arithmetic, per_device(): values = jnp.where(is_live[:, None], values, jnp.zeros_like(values))  15.2 us
  transfers between devices with their start and end apart: 7, of which 5 were waited for; matrix products, arithmetic and copies ran while one was open for 39% of the time, Pallas kernels for 0%

commit v1 on v0

--- a/solution.py
+++ b/solution.py
@@ -122,7 +122,7 @@
     aligned = jnp.concatenate(window_rows, axis=0).astype(jnp.bfloat16)
     cal_rows = gather_all_axes(calibration, TM, 0)
     running = jnp.dot(
-        lax.all_gather(aligned, "col", axis=1, tiled=True),
+        jnp.concatenate(lax.all_gather(aligned, "col"), axis=1),
         cal_rows,
         preferred_element_type=jnp.float32,
     )

time: 364 us -> 386 us (1.060)
  local copies, waits for them, and re-layouts: 46.6 us -> 68.1 us
    all_gather x0 -> x1, local copies, waits for them, and re-layouts: none -> 21.6 us  [per_device(): lax.all_gather(aligned, 'col')]
  transfers between devices with their start and end apart: 7 -> 7, of which waited for: 5 -> 5; matrix products, arithmetic and copies ran while one was open for 39% -> 37% of each run, Pallas kernels for 0% -> 0%
where the time goes in v1:
time: 386 us; the launch traced here: 381 us
  waiting for transfers between devices  171 us (44%)
  local copies, waits for them, and re-layouts  68.1 us (18%)
  matrix products  62.8 us (16%)
  other arithmetic  51.4 us (13%)
  between operations  14.5 us (4%)
  starting transfers between devices  12.6 us (3%)
    all_gather x4, waiting for transfers between devices, gather_in_order(): parts = lax.all_gather(parts, axes[k], axis=0, tiled=True)  77.1 us
    all_gather x1, waiting for transfers between devices, per_device(): lax.all_gather(aligned, 'col')  72.7 us
    dot_general x4, matrix products, per_device(): lax.dot_general(upper_part, place_onehot, dims, preferred_element_type=jn...  21.8 us
    all_gather x1, local copies, waits for them, and re-layouts, per_device(): lax.all_gather(aligned, 'col')  21.6 us
    dot_general x4, matrix products, per_device(): lax.dot_general(lower_part, place_onehot, dims, preferred_element_type=jn...  21.5 us
    all_to_all x1, waiting for transfers between devices, per_device(): lax.all_to_all(outgoing, TM, split_axis=0, concat_axis=0, tiled=True)  20.8 us
    dot_general x1, matrix products, per_device(): jnp.dot(jnp.concatenate(lax.all_gather(aligned, 'col'), axis=1), cal_rows...  18 us
    gather x1, local copies, waits for them, and re-layouts, per_device(): jnp.take(row_keys, source_row, axis=0)  17.4 us
  transfers between devices with their start and end apart: 7, of which 5 were waited for; matrix products, arithmetic and copies ran while one was open for 37% of the time, Pallas kernels for 0%

profile of v1, /device:TPU:1, one launch (start us, length us, event | category | flops | bytes accessed | tf_op | source)
XLA Modules:
  0.0 380.7 jit_solution(2134983533075024467)
XLA Ops:
  6.5 0.0 copy-start.2
  6.5 0.0 all-gather.16.cloned.1.call-start
  6.5 2.3 fusion.49
  8.8 0.0 all-gather.16.cloned.1.call-update
  8.8 0.0 all-gather.14.cloned.1.call-start
  8.9 0.7 all-gather.14.cloned.1.call-update
  9.6 0.0 all-gather.12.cloned.1.call-start
  9.6 33.4 %all-gather.16.cloned.1.call-done = bf16[2048,512]{1,0:T(8,128)(2,1)} async-done(((bf16[512,512]{1,0:T(8,128)(2,1)}), bf16[2048,512]{1,0:T(8,128)(2,1)}) %all-gather.16.cloned.1.call-update) | async-done | bytes 2097168 | tf_op jit(solution)/shard_map/all_gather | solution.py:20
  43.1 0.0 all-gather.12.cloned.1.call-update
  43.1 0.0 copy-start.3
  43.1 0.0 copy-start.4
  43.1 0.0 all-gather.10.cloned.1.call-start
  43.2 32.3 %all-gather.14.cloned.1.call-done = bf16[2048,512]{1,0:T(8,128)(2,1)} async-done(((bf16[512,512]{1,0:T(8,128)(2,1)}), bf16[2048,512]{1,0:T(8,128)(2,1)}) %all-gather.14.cloned.1.call-update) | async-done | bytes 2097168 | tf_op jit(solution)/shard_map/all_gather | solution.py:20
  75.4 0.0 all-gather.10.cloned.1.call-update
  75.4 0.0 copy-done.2
  75.4 1.5 fusion.42
  77.0 3.4 select_reduce_fusion
  80.4 0.0 copy-done.3
  80.4 0.0 copy-done.4
  80.4 0.0 copy-start
  80.4 0.0 copy-start.1
  80.4 17.4 %gather_fusion.1 = s32[3072]{0:T(1024)S(1)} fusion(s32[2048]{0:T(1024)S(1)} %bitcast.48, s32[3072]{0:T(1024)S(1)} %maximum_clamp_fusion), kind=kCustom, calls=%fused_computation.1 | custom fusion | bytes 36864 | tf_op jit(solution)/shard_map/jit(_take)/gather | solution.py:98
  97.9 0.7 select_n.64
  98.5 5.7 %all-to-all-start.1 = ((s32[16,1,192]{2,1,0:T(1,128)}), s32[16,1,192]{2,1,0:T(1,128)S(1)}, u32[]{:S(2)}, u32[]{:S(2)}) async-start(s32[16,1,192]{2,1,0:T(1,128)} %select_n.64), calls=%async_computation.1 | async-start | bytes 32768 | tf_op jit(solution)/shard_map/all_to_all | solution.py:104
  104.9 0.1 le.30
  104.9 0.1 ge.33
  105.0 0.0 copy-done
  105.0 8.1 %copy.23 = bf16[2048,1,128]{2,1,0:T(2,128)(2,1)S(1)} copy(bf16[2048,1,128]{2,0,1:T(8,128)(2,1)S(1)} %bitcast.58) | data formatting | bytes 1048576 | tf_op jit(solution)/shard_map/stack;squeeze | solution.py:93
  113.2 0.0 copy-done.1
  113.2 15.2 %broadcast_select_fusion.2 = bf16[2048,1,128]{2,1,0:T(2,128)(2,1)S(1)} fusion(pred[2048]{0:T(1024)(128)(4,1)S(1)} %iota_compare_fusion.45, bf16[2048,1,128]{2,0,1:T(8,128)(2,1)S(1)} %bitcast.59), kind=kLoop, calls=%fused_computation.46 | loop fusion | flops 262144 | bytes 1050624 | tf_op jit(solution)/shard_map/jit(_where)/select_n | solution.py:81
  128.4 2.4 pad_maximum_fusion.2
  130.8 10.4 %gather_fusion = bf16[3072,2,128]{2,1,0:T(2,128)(2,1)S(1)} fusion(bf16[2048,2,128]{2,1,0:T(2,128)(2,1)S(1)} %pad_maximum_fusion.2, s32[3072]{0:T(1024)S(1)} %maximum_clamp_fusion), kind=kCustom, calls=%fused_computation | custom fusion | bytes 3158016 | tf_op jit(solution)/shard_map/jit(_take)/gather | solution.py:95
  141.3 9.9 %broadcast_select_fusion.1 = bf16[16,192,2,128]{3,2,1,0:T(2,128)(2,1)} fusion(pred[16,192]{1,0:T(8,128)(4,1)S(1)} %ge.33, bf16[16,192,2,128]{3,2,1,0:T(2,128)(2,1)S(1)} %bitcast.55, pred[16,192]{1,0:T(8,128)(4,1)S(1)} %le.30), kind=kLoop, calls=%fused_computation.28 | loop fusion | flops 1572864 | bytes 3151872 | tf_op jit(solution)/shard_map/jit(_where)/select_n | solution.py:94
  151.2 0.0 all-to-all-done.1
  151.2 6.8 %all-to-all-start = ((bf16[16,192,2,128]{3,2,1,0:T(2,128)(2,1)}), bf16[16,192,2,128]{3,2,1,0:T(2,128)(2,1)S(1)}, u32[]{:S(2)}, u32[]{:S(2)}) async-start(bf16[16,192,2,128]{3,2,1,0:T(2,128)(2,1)} %broadcast_select_fusion.1), calls=%async_computation | async-start | bytes 3145728 | tf_op jit(solution)/shard_map/all_to_all | solution.py:102
  158.0 0.0 all-gather.8.cloned.1.call-start
  158.1 0.1 eq.36
  158.1 20.8 %all-to-all-done = bf16[16,192,2,128]{3,2,1,0:T(2,128)(2,1)S(1)} async-done(((bf16[16,192,2,128]{3,2,1,0:T(2,128)(2,1)}), bf16[16,192,2,128]{3,2,1,0:T(2,128)(2,1)S(1)}, u32[]{:S(2)}, u32[]{:S(2)}) %all-to-all-start) | async-done | bytes 1572896 | tf_op jit(solution)/shard_map/all_to_all | solution.py:102
  178.9 2.6 fusion.48
  181.5 0.8 fusion.45
  182.3 0.8 slice_multiply_fusion.1
  183.1 0.7 pad_add_fusion
  183.8 0.2 fusion.41
  184.0 5.3 %fusion.6 = f32[128,2048]{1,0:T(8,128)S(1)} fusion(bf16[3072,128]{1,0:T(8,128)(2,1)S(1)} %get-tuple-element.8, s32[3072]{0:T(1024)S(1)} %eq.36), kind=kOutput, calls=%fused_computation.12 | convolution fusion | flops 1616904192 | bytes 1847296 | tf_op jit(solution)/shard_map/dot_general | solution.py:118
  189.4 5.3 %fusion = f32[128,2048]{1,0:T(8,128)S(1)} fusion(bf16[3072,128]{1,0:T(8,128)(2,1)S(1)} %get-tuple-element.8, s32[3072]{0:T(1024)S(1)} %get-tuple-element.20), kind=kOutput, calls=%fused_computation.3 | convolution fusion | flops 1616904192 | bytes 1847296 | tf_op jit(solution)/shard_map/dot_general | solution.py:118
  194.7 5.5 %fusion.2 = f32[128,2048]{1,0:T(8,128)S(1)} fusion(bf16[3072,128]{1,0:T(8,128)(2,1)S(1)} %get-tuple-element.8, s32[3072]{0:T(1024)S(1)} %get-tuple-element.21), kind=kOutput, calls=%fused_computation.6 | convolution fusion | flops 1616904192 | bytes 1847296 | tf_op jit(solution)/shard_map/dot_general | solution.py:118
  200.2 5.3 %fusion.4 = f32[128,2048]{1,0:T(8,128)S(1)} fusion(bf16[3072,128]{1,0:T(8,128)(2,1)S(1)} %get-tuple-element.8, s32[3072]{0:T(1024)S(1)} %get-tuple-element.19), kind=kOutput, calls=%fused_computation.9 | convolution fusion | flops 1616904192 | bytes 1847296 | tf_op jit(solution)/shard_map/dot_general | solution.py:118
  205.5 5.5 %fusion.28 = bf16[1,128,2048]{2,1,0:T(8,128)(2,1)S(1)} fusion(f32[128,2048]{1,0:T(8,128)S(1)} %fusion, bf16[3072,128]{1,0:T(8,128)(2,1)S(1)} %get-tuple-element.9, s32[3072]{0:T(1024)S(1)} %get-tuple-element.20), kind=kOutput, calls=%fused_computation.43 | convolution fusion | flops 1617428480 | bytes 2371584 | tf_op jit(solution)/shard_map/dot_general | solution.py:115
  211.1 5.3 %fusion.27 = bf16[1,128,2048]{2,1,0:T(8,128)(2,1)S(1)} fusion(f32[128,2048]{1,0:T(8,128)S(1)} %fusion.2, bf16[3072,128]{1,0:T(8,128)(2,1)S(1)} %get-tuple-element.9, s32[3072]{0:T(1024)S(1)} %get-tuple-element.21), kind=kOutput, calls=%fused_computation.42 | convolution fusion | flops 1617428480 | bytes 2371584 | tf_op jit(solution)/shard_map/dot_general | solution.py:115
  216.4 5.3 %fusion.26 = bf16[1,128,2048]{2,1,0:T(8,128)(2,1)S(1)} fusion(f32[128,2048]{1,0:T(8,128)S(1)} %fusion.4, bf16[3072,128]{1,0:T(8,128)(2,1)S(1)} %get-tuple-element.9, s32[3072]{0:T(1024)S(1)} %get-tuple-element.19), kind=kOutput, calls=%fused_computation.41 | convolution fusion | flops 1617428480 | bytes 2371584 | tf_op jit(solution)/shard_map/dot_general | solution.py:115
  221.8 5.6 %fusion.25 = bf16[1,128,2048]{2,1,0:T(8,128)(2,1)S(1)} fusion(f32[128,2048]{1,0:T(8,128)S(1)} %fusion.6, bf16[3072,128]{1,0:T(8,128)(2,1)S(1)} %get-tuple-element.9, s32[3072]{0:T(1024)S(1)} %eq.36), kind=kOutput, calls=%fused_computation.40 | convolution fusion | flops 1617428480 | bytes 2371584 | tf_op jit(solution)/shard_map/dot_general | solution.py:115
  227.4 1.4 pad_maximum_fusion.1
  228.8 0.0 all-gather.8.cloned.1.call-update
  228.8 0.0 all-gather.12.cloned.1.call-done
  228.9 7.3 %copy.26 = bf16[4,4,512,512]{3,2,0,1:T(8,128)(2,1)} copy(bf16[4,4,512,512]{3,2,1,0:T(8,128)(2,1)} %bitcast.54) | data formatting | bytes 16777216 | tf_op jit(solution)/shard_map/reshape | solution.py:22
  236.2 11.3 %all-gather.10.cloned.1.call-done = bf16[16,512,512]{2,1,0:T(8,128)(2,1)} async-done(((bf16[4,512,512]{2,1,0:T(8,128)(2,1)}), bf16[16,512,512]{2,1,0:T(8,128)(2,1)}) %all-gather.10.cloned.1.call-update) | async-done | bytes 8388624 | tf_op jit(solution)/shard_map/all_gather | solution.py:20
  247.6 13.9 %pad_maximum_fusion = bf16[16,1024,512]{2,1,0:T(8,128)(2,1)} fusion(bf16[16,512,512]{2,1,0:T(8,128)(2,1)} %bitcast.49, bf16[16,512,512]{2,1,0:T(8,128)(2,1)} %all-gather.10.cloned.1.call-done), kind=kLoop, calls=%fused_computation.16 | loop fusion | flops 33554432 | bytes 33554432 | tf_op jit(solution)/shard_map/concatenate | solution.py:42
  261.4 72.7 %all-gather.8.cloned.1.call-done = bf16[8,512,2048]{2,1,0:T(8,128)(2,1)} async-done(((bf16[1,512,2048]{2,1,0:T(8,128)(2,1)}), bf16[8,512,2048]{2,1,0:T(8,128)(2,1)}) %all-gather.8.cloned.1.call-update) | async-done | bytes 16777232 | tf_op jit(solution)/shard_map/all_gather | solution.py:125
  334.1 21.6 %copy.25 = bf16[8,512,2048]{1,2,0:T(8,128)(2,1)} copy(bf16[8,512,2048]{2,1,0:T(8,128)(2,1)} %all-gather.8.cloned.1.call-done) | data formatting | bytes 33554432 | tf_op jit(solution)/shard_map/all_gather | solution.py:125
  355.7 18.0 %convolution_convert_fusion = bf16[512,512]{1,0:T(8,128)(2,1)} fusion(bf16[512,16384]{0,1:T(8,128)(2,1)} %bitcast.53, bf16[16384,512]{1,0:T(8,128)(2,1)} %bitcast.52), kind=kOutput, calls=%fused_computation.65 | convolution fusion | flops 8590196736 | bytes 34078720 | tf_op jit(solution)/shard_map/dot_general | solution.py:124
  (7 shorter events, 0.1 us)
Async XLA Ops:
  6.5 68.9 %copy-start.2 = (s32[1,2048,1]{1,2,0:T(1,128)S(1)}, s32[1,2048,1]{1,2,0:T(1,128)}, u32[]{:S(2)}) copy-start(s32[1,2048,1]{1,2,0:T(1,128)} %param.11) | copy-start | bytes 24580
  6.5 36.5 %all-gather.16.cloned.1.call-start = ((), (), s32[]{:S(2)}) async-start(), calls=%async_computation.6 | async-start | bytes 2621440 | tf_op jit(solution)/shard_map/all_gather | solution.py:20
  8.8 66.6 %all-gather.14.cloned.1.call-start = ((), (), s32[]{:S(2)}) async-start(), calls=%async_computation.5 | async-start | bytes 2621440 | tf_op jit(solution)/shard_map/all_gather | solution.py:20
  9.6 219.3 %all-gather.12.cloned.1.call-start = ((), (), s32[]{:S(2)}) async-start(), calls=%async_computation.4 | async-start | bytes 10485760 | tf_op jit(solution)/shard_map/all_gather | solution.py:20
  43.1 37.3 %copy-start.3 = (s32[1,2048]{1,0:T(1,128)S(1)}, s32[1,2048]{1,0:T(1,128)}, u32[]{:S(2)}) copy-start(s32[1,2048]{1,0:T(1,128)} %param.9) | copy-start | bytes 24580
  43.1 37.3 %copy-start.4 = (s32[1,2048]{1,0:T(1,128)S(1)}, s32[1,2048]{1,0:T(1,128)}, u32[]{:S(2)}) copy-start(s32[1,2048]{1,0:T(1,128)} %param.10) | copy-start | bytes 24580
  43.1 204.5 %all-gather.10.cloned.1.call-start = ((), (), s32[]{:S(2)}) async-start(), calls=%async_computation.3 | async-start | bytes 10485760 | tf_op jit(solution)/shard_map/all_gather | solution.py:20
  80.4 24.6 %copy-start = (bf16[1,2048,128]{2,1,0:T(8,128)(2,1)S(1)}, bf16[1,2048,128]{2,1,0:T(8,128)(2,1)}, u32[]{:S(2)}) copy-start(bf16[1,2048,128]{2,1,0:T(8,128)(2,1)} %param.8) | copy-start | bytes 1572868
  80.4 32.8 %copy-start.1 = (bf16[1,2048,128]{2,1,0:T(8,128)(2,1)S(1)}, bf16[1,2048,128]{2,1,0:T(8,128)(2,1)}, u32[]{:S(2)}) copy-start(bf16[1,2048,128]{2,1,0:T(8,128)(2,1)} %param.7) | copy-start | bytes 1572868
  98.5 52.6 %all-to-all-start.1 = ((s32[16,1,192]{2,1,0:T(1,128)}), s32[16,1,192]{2,1,0:T(1,128)S(1)}, u32[]{:S(2)}, u32[]{:S(2)}) async-start(s32[16,1,192]{2,1,0:T(1,128)} %select_n.64), calls=%async_computation.1 | async-start | bytes 32768 | tf_op jit(solution)/shard_map/all_to_all | solution.py:104
  151.2 27.7 %all-to-all-start = ((bf16[16,192,2,128]{3,2,1,0:T(2,128)(2,1)}), bf16[16,192,2,128]{3,2,1,0:T(2,128)(2,1)S(1)}, u32[]{:S(2)}, u32[]{:S(2)}) async-start(bf16[16,192,2,128]{3,2,1,0:T(2,128)(2,1)} %broadcast_select_fusion.1), calls=%async_computation | async-start | bytes 3145728 | tf_op jit(solution)/shard_map/all_to_all | solution.py:102
  158.0 176.2 %all-gather.8.cloned.1.call-start = ((), (), s32[]{:S(2)}) async-start(), calls=%async_computation.2 | async-start | bytes 18874368 | tf_op jit(solution)/shard_map/all_gather | solution.py:125
Sparse Core Ops, SparseCore 0:
  9.0 34.0 all-gather.15
  44.7 30.6 all-gather.13
  77.1 83.2 all-gather.11
  161.9 85.6 all-gather.9
  249.1 84.9 all-gather.7
